TPU v7x, 32 devices: a whole 2x2x4 slice. The times are simulated.
32 devices in a mesh: dp: 8 (over z, y), tensor: 4 (over x, core).
Axes of the slice: x: 2, y: 2, z: 4, core: 2. Of those that a mesh axis runs over, the one named last changes fastest.
Arguments:
- block_input: bfloat16 [2, 1024, 8, 1024], P(None, 'tensor', 'dp'), may hold values from -6 to 6
- qkv_weight: bfloat16 [1024, 3, 1024], P('dp', None, 'tensor'), may hold values from -0.1875 to 0.1875
- qv_bias: float32 [2, 1024], P(None, 'tensor'), may hold values from -2 to 2
- out_weight: bfloat16 [1024, 1024], P('dp', 'tensor'), may hold values from -0.75 to 0.75
- out_bias: float32 [1024], replicated, may hold values from -2 to 2
- fc_weight: bfloat16 [1024, 4096], P('dp', 'tensor'), may hold values from -0.1875 to 0.1875
- fc_bias: float32 [4096], P('tensor'), may hold values from -2 to 2
- proj_weight: bfloat16 [1024, 4096], P('dp', 'tensor'), may hold values from -0.09375 to 0.09375
- proj_bias: float32 [1024], replicated, may hold values from -2 to 2
- norm1_gain: float32 [1024], replicated, may hold values from 0.1 to 1.9
- norm1_shift: float32 [1024], replicated, may hold values from -2 to 2
- norm2_gain: float32 [1024], replicated, may hold values from 0.1 to 1.9
- norm2_shift: float32 [1024], replicated, may hold values from -2 to 2
- out_grad: bfloat16 [2, 1024, 8, 1024], P(None, 'tensor', 'dp'), may hold values from -6 to 6
Outputs:
- block_output: bfloat16 [2, 1024, 8, 1024], P(None, 'tensor', 'dp')
- input_grad: bfloat16 [2, 1024, 8, 1024], P(None, 'tensor', 'dp')
- qkv_weight_grad: float32 [1024, 3, 1024], P('dp', None, 'tensor')
- qv_bias_grad: float32 [2, 1024], P(None, 'tensor')
- out_weight_grad: float32 [1024, 1024], P('dp', 'tensor')
- out_bias_grad: float32 [1024], replicated
- fc_weight_grad: float32 [1024, 4096], P('dp', 'tensor')
- fc_bias_grad: float32 [4096], P('tensor')
- proj_weight_grad: float32 [1024, 4096], P('dp', 'tensor')
- proj_bias_grad: float32 [1024], replicated
- norm1_gain_grad: float32 [1024], replicated
- norm1_shift_grad: float32 [1024], replicated
- norm2_gain_grad: float32 [1024], replicated
- norm2_shift_grad: float32 [1024], replicated
All inputs are finite; a program needn't handle non-finite values.
Results may differ from a plain program's by a relative error of at most 0.012.
Values may be sent and summed in bfloat16 or wider, within the bound.
A program may use at most 128 MiB of HBM per device.

v0:
```python
import jax
import jax.numpy as jnp
from jax import lax
from jax.sharding import PartitionSpec as P

HEAD_DIM = 64
norm_eps = 1e-05
tanh_coef = 0.7978845608028654
cube_coef = 0.044715
block_rows = 512


def gelu_tanh(values):
    return (
        0.5 * values * (1.0 + jnp.tanh(tanh_coef * (values + cube_coef * values * values * values)))
    )


def norm_parts(rows):
    center = rows - jnp.mean(rows, axis=-1, keepdims=True)
    spread = jnp.mean(center * center, axis=-1, keepdims=True)
    inverse = lax.rsqrt(spread + norm_eps)
    return (center * inverse, inverse)


def norm_back(grad_out, normed, inverse, gain):
    grad_normed = grad_out * gain
    first = jnp.mean(grad_normed, axis=-1, keepdims=True)
    second = jnp.mean(grad_normed * normed, axis=-1, keepdims=True)
    return inverse * (grad_normed - first - normed * second)


def causal_scores(query_block, keys, offset):
    scores = jnp.einsum(
        "qbhe,kbhe->bhqk", query_block, keys, preferred_element_type=jnp.float32
    ) * HEAD_DIM ** (-0.5)
    height = query_block.shape[0]
    length = keys.shape[0]
    row_pos = lax.broadcasted_iota(jnp.int32, (height, length), 0) + offset
    col_pos = lax.broadcasted_iota(jnp.int32, (height, length), 1)
    return jnp.where(col_pos <= row_pos, scores, -1e30)


def attend_forward(queries, keys, values):
    length = keys.shape[0]
    span = min(block_rows, length)
    outputs = []
    totals = []
    for offset in range(0, length, span):
        scores = causal_scores(queries[offset : offset + span], keys, offset)
        peak = jnp.max(scores, axis=-1, keepdims=True)
        raised = jnp.exp(scores - peak)
        total = jnp.sum(raised, axis=-1, keepdims=True)
        weights = (raised / total).astype(jnp.bfloat16)
        outputs.append(
            jnp.einsum("bhqk,kbhe->qbhe", weights, values, preferred_element_type=jnp.float32)
        )
        totals.append(peak + jnp.log(total))
    return (jnp.concatenate(outputs, 0), jnp.concatenate(totals, 2))


def attend_backward(queries, keys, values, log_totals, grad_out):
    length = keys.shape[0]
    span = min(block_rows, length)
    scale = HEAD_DIM ** (-0.5)
    grad_queries = []
    grad_keys = jnp.zeros(keys.shape, jnp.float32)
    grad_values = jnp.zeros(values.shape, jnp.float32)
    for offset in range(0, length, span):
        query_block = queries[offset : offset + span]
        grad_block = grad_out[offset : offset + span]
        scores = causal_scores(query_block, keys, offset)
        probs = jnp.exp(scores - log_totals[:, :, offset : offset + span])
        grad_probs = jnp.einsum(
            "qbhe,kbhe->bhqk", grad_block, values, preferred_element_type=jnp.float32
        )
        inner = jnp.sum(probs * grad_probs, axis=-1, keepdims=True)
        grad_scores = (probs * (grad_probs - inner)).astype(jnp.bfloat16)
        grad_queries.append(
            jnp.einsum("bhqk,kbhe->qbhe", grad_scores, keys, preferred_element_type=jnp.float32)
            * scale
        )
        grad_keys = (
            grad_keys
            + jnp.einsum(
                "bhqk,qbhe->kbhe", grad_scores, query_block, preferred_element_type=jnp.float32
            )
            * scale
        )
        grad_values = grad_values + jnp.einsum(
            "bhqk,qbhe->kbhe",
            probs.astype(jnp.bfloat16),
            grad_block,
            preferred_element_type=jnp.float32,
        )
    return (jnp.concatenate(grad_queries, 0), grad_keys, grad_values)


def per_device(
    block_input,
    qkv_weight,
    qv_bias,
    out_weight,
    out_bias,
    fc_weight,
    fc_bias,
    proj_weight,
    proj_bias,
    norm1_gain,
    norm1_shift,
    norm2_gain,
    norm2_shift,
    out_grad,
):
    micro = block_input.shape[0]
    heads_local = qkv_weight.shape[2] // HEAD_DIM
    rows = qkv_weight.shape[0]
    width_qkv = qkv_weight.shape[1] * qkv_weight.shape[2]
    width_out = out_weight.shape[1]
    width_fc = fc_weight.shape[1]
    cuts = (width_qkv, width_qkv + width_out, width_qkv + width_out + width_fc)
    packed = jnp.concatenate(
        [qkv_weight.reshape(rows, width_qkv), out_weight, fc_weight, proj_weight], axis=1
    )
    packed_full = lax.all_gather(packed, "dp", axis=0, tiled=True)
    depth = packed_full.shape[0]
    qkv_full = packed_full[:, : cuts[0]].reshape(depth, 3, qkv_weight.shape[2])
    out_full = packed_full[:, cuts[0] : cuts[1]]
    fc_full = packed_full[:, cuts[1] : cuts[2]]
    proj_full = packed_full[:, cuts[2] :]
    grad_top_all = lax.all_gather(out_grad, "tensor", axis=1, tiled=True)
    weight_init = jnp.zeros(packed_full.shape, jnp.float32)
    small_init = (
        jnp.zeros(qv_bias.shape, jnp.float32),
        jnp.zeros(fc_bias.shape, jnp.float32),
        jnp.zeros(out_bias.shape, jnp.float32),
        jnp.zeros(proj_bias.shape, jnp.float32),
        jnp.zeros(norm1_gain.shape, jnp.float32),
        jnp.zeros(norm1_shift.shape, jnp.float32),
        jnp.zeros(norm2_gain.shape, jnp.float32),
        jnp.zeros(norm2_shift.shape, jnp.float32),
    )
    outputs_init = jnp.zeros(block_input.shape, jnp.bfloat16)
    in_grads_init = jnp.zeros(block_input.shape, jnp.bfloat16)

    def one_micro(index, carry):
        outputs_all, in_grads_all, weight_acc, small_acc = carry
        resid_in = lax.dynamic_index_in_dim(block_input, index, 0, keepdims=False).astype(
            jnp.float32
        )
        grad_top = lax.dynamic_index_in_dim(out_grad, index, 0, keepdims=False)
        grad_top_full = lax.dynamic_index_in_dim(grad_top_all, index, 0, keepdims=False)
        normed1, inverse1 = norm_parts(resid_in)
        hidden1 = (normed1 * norm1_gain + norm1_shift).astype(jnp.bfloat16)
        hidden1_full = lax.all_gather(hidden1, "tensor", axis=0, tiled=True)
        length = hidden1_full.shape[0]
        batch = hidden1_full.shape[1]
        projected = jnp.einsum(
            "lbd,dce->lbce", hidden1_full, qkv_full, preferred_element_type=jnp.float32
        )
        qkv_bias = jnp.stack([qv_bias[0], jnp.zeros_like(qv_bias[0]), qv_bias[1]])
        qkv_values = (projected + qkv_bias).astype(jnp.bfloat16)
        split = qkv_values.reshape(length, batch, 3, heads_local, HEAD_DIM)
        queries = split[:, :, 0]
        keys = split[:, :, 1]
        values = split[:, :, 2]
        attended, log_totals = attend_forward(queries, keys, values)
        mixed = attended.astype(jnp.bfloat16).reshape(length, batch, heads_local * HEAD_DIM)
        attn_branch = lax.psum_scatter(
            jnp.einsum("lbi,oi->lbo", mixed, out_full, preferred_element_type=jnp.float32),
            "tensor",
            scatter_dimension=0,
            tiled=True,
        )
        middle = resid_in + attn_branch + out_bias
        normed2, inverse2 = norm_parts(middle)
        hidden2 = (normed2 * norm2_gain + norm2_shift).astype(jnp.bfloat16)
        hidden2_full = lax.all_gather(hidden2, "tensor", axis=0, tiled=True)
        pre_act = (
            jnp.einsum("lbd,df->lbf", hidden2_full, fc_full, preferred_element_type=jnp.float32)
            + fc_bias
        )
        activated = gelu_tanh(pre_act).astype(jnp.bfloat16)
        mlp_branch = lax.psum_scatter(
            jnp.einsum(
                "lbf,of->lbo", activated, proj_full, preferred_element_type=jnp.float32
            ).astype(jnp.bfloat16),
            "tensor",
            scatter_dimension=0,
            tiled=True,
        ).astype(jnp.float32)
        block_out = (middle + mlp_branch + proj_bias).astype(jnp.bfloat16)
        grad_proj = jnp.einsum(
            "lbo,lbf->of", grad_top_full, activated, preferred_element_type=jnp.float32
        )
        grad_act = jnp.einsum(
            "lbo,of->lbf", grad_top_full, proj_full, preferred_element_type=jnp.float32
        )
        _, gelu_pull = jax.vjp(gelu_tanh, pre_act)
        grad_pre = gelu_pull(grad_act)[0].astype(jnp.bfloat16)
        grad_fc_bias = jnp.sum(grad_pre.astype(jnp.float32), axis=(0, 1))
        grad_fc = jnp.einsum(
            "lbd,lbf->df", hidden2_full, grad_pre, preferred_element_type=jnp.float32
        )
        grad_h2 = lax.psum_scatter(
            jnp.einsum("lbf,df->lbd", grad_pre, fc_full, preferred_element_type=jnp.float32),
            "tensor",
            scatter_dimension=0,
            tiled=True,
        )
        grad_gain2 = jnp.sum(grad_h2 * normed2, axis=(0, 1))
        grad_shift2 = jnp.sum(grad_h2, axis=(0, 1))
        grad_mid = grad_top.astype(jnp.float32) + norm_back(grad_h2, normed2, inverse2, norm2_gain)
        grad_out_bias = jnp.sum(grad_mid, axis=(0, 1))
        grad_proj_bias = jnp.sum(grad_top.astype(jnp.float32), axis=(0, 1))
        grad_mid_full = lax.all_gather(grad_mid.astype(jnp.bfloat16), "tensor", axis=0, tiled=True)
        grad_out_w = jnp.einsum(
            "lbo,lbi->oi", grad_mid_full, mixed, preferred_element_type=jnp.float32
        )
        grad_mixed = jnp.einsum(
            "lbo,oi->lbi", grad_mid_full, out_full, preferred_element_type=jnp.float32
        )
        grad_mixed = grad_mixed.astype(jnp.bfloat16).reshape(length, batch, heads_local, HEAD_DIM)
        grad_queries, grad_keys, grad_values = attend_backward(
            queries, keys, values, log_totals, grad_mixed
        )
        grad_qkv = jnp.stack([grad_queries, grad_keys, grad_values], axis=2).astype(jnp.bfloat16)
        grad_qkv = grad_qkv.reshape(length, batch, 3, heads_local * HEAD_DIM)
        kind_sums = jnp.sum(grad_qkv.astype(jnp.float32), axis=(0, 1))
        grad_qv_bias = jnp.stack([kind_sums[0], kind_sums[2]])
        grad_qkv_w = jnp.einsum(
            "lbd,lbce->dce", hidden1_full, grad_qkv, preferred_element_type=jnp.float32
        )
        grad_h1 = lax.psum_scatter(
            jnp.einsum("lbce,dce->lbd", grad_qkv, qkv_full, preferred_element_type=jnp.float32),
            "tensor",
            scatter_dimension=0,
            tiled=True,
        )
        grad_gain1 = jnp.sum(grad_h1 * normed1, axis=(0, 1))
        grad_shift1 = jnp.sum(grad_h1, axis=(0, 1))
        grad_in = (grad_mid + norm_back(grad_h1, normed1, inverse1, norm1_gain)).astype(
            jnp.bfloat16
        )
        fresh_weights = jnp.concatenate(
            [grad_qkv_w.reshape(depth, width_qkv), grad_out_w, grad_fc, grad_proj], axis=1
        )
        weight_acc = weight_acc + fresh_weights
        fresh = (
            grad_qv_bias,
            grad_fc_bias,
            grad_out_bias,
            grad_proj_bias,
            grad_gain1,
            grad_shift1,
            grad_gain2,
            grad_shift2,
        )
        small_acc = tuple((total + extra for total, extra in zip(small_acc, fresh)))
        outputs_all = lax.dynamic_update_index_in_dim(outputs_all, block_out, index, 0)
        in_grads_all = lax.dynamic_update_index_in_dim(in_grads_all, grad_in, index, 0)
        return (outputs_all, in_grads_all, weight_acc, small_acc)

    outputs_all, in_grads_all, weight_acc, small_acc = lax.fori_loop(
        0, micro, one_micro, (outputs_init, in_grads_init, weight_init, small_init)
    )
    weight_shard = lax.psum_scatter(weight_acc, "dp", scatter_dimension=0, tiled=True)
    grad_qkv_w = weight_shard[:, : cuts[0]].reshape(qkv_weight.shape)
    grad_out_w = weight_shard[:, cuts[0] : cuts[1]]
    grad_fc_w = weight_shard[:, cuts[1] : cuts[2]]
    grad_proj_w = weight_shard[:, cuts[2] :]
    tensor_size = lax.psum(1, "tensor")
    slot = lax.axis_index("tensor")
    head_vec = jnp.concatenate([small_acc[0].reshape(-1), small_acc[1]])
    head_slots = jnp.zeros((tensor_size, head_vec.shape[0]), jnp.float32)
    head_slots = lax.dynamic_update_index_in_dim(head_slots, head_vec, slot, 0)
    feature_vec = jnp.concatenate([item for item in small_acc[2:]])
    total = lax.psum(jnp.concatenate([feature_vec, head_slots.reshape(-1)]), ("dp", "tensor"))
    features = total[: feature_vec.shape[0]].reshape(6, -1)
    head_total = lax.dynamic_index_in_dim(
        total[feature_vec.shape[0] :].reshape(tensor_size, -1), slot, 0, keepdims=False
    )
    qv_size = small_acc[0].size
    grad_qv_bias = head_total[:qv_size].reshape(small_acc[0].shape)
    grad_fc_bias = head_total[qv_size:]
    return (
        outputs_all,
        in_grads_all,
        grad_qkv_w,
        grad_qv_bias,
        grad_out_w,
        features[0],
        grad_fc_w,
        grad_fc_bias,
        grad_proj_w,
        features[1],
        features[2],
        features[3],
        features[4],
        features[5],
    )


def solution(mesh):
    in_specs = (
        P(None, "tensor", "dp", None),
        P("dp", None, "tensor"),
        P(None, "tensor"),
        P("dp", "tensor"),
        P(),
        P("dp", "tensor"),
        P("tensor"),
        P("dp", "tensor"),
        P(),
        P(),
        P(),
        P(),
        P(),
        P(None, "tensor", "dp", None),
    )
    out_specs = (
        P(None, "tensor", "dp", None),
        P(None, "tensor", "dp", None),
        P("dp", None, "tensor"),
        P(None, "tensor"),
        P("dp", "tensor"),
        P(),
        P("dp", "tensor"),
        P("tensor"),
        P("dp", "tensor"),
        P(),
        P(),
        P(),
        P(),
        P(),
    )
    return jax.shard_map(
        per_device, mesh=mesh, in_specs=in_specs, out_specs=out_specs, check_vma=False
    )
```

profile of v0, /device:TPU:0, one launch (start us, length us, event | category | flops | bytes accessed | tf_op | source)
XLA Modules:
  0.0 999.4 jit_solution(10423390227295797122)
XLA Ops:
  13.4 101.5 %all-gather.6.cloned.1.call-done = bf16[1024,3072]{0,1:T(8,128)(2,1)} async-done(((bf16[128,3072]{0,1:T(8,128)(2,1)}), bf16[1024,3072]{0,1:T(8,128)(2,1)}) %all-gather.6.cloned.1.call-update) | async-done | bytes 6291472 | tf_op jit(solution)/shard_map/all_gather | solution.py:125
  130.1 19.0 %all-gather.8.cloned.1.call-done = bf16[2,1024,1,1024]{3,1,2,0:T(8,128)(2,1)} async-done(((bf16[2,256,1,1024]{3,1,2,0:T(8,128)(2,1)}), bf16[2,1024,1,1024]{3,1,2,0:T(8,128)(2,1)}) %all-gather.8.cloned.1.call-update) | async-done | bytes 4194320 | tf_op jit(solution)/shard_map/all_gather | solution.py:131
  149.1 623.7 %while.34 = (s32[]{:T(128)}, bf16[2,256,1,1024]{3,1,2,0:T(8,128)(2,1)}, bf16[2,256,1,1024]{3,1,2,0:T(8,128)(2,1)}, f32[1024,3072]{0,1:T(8,128)}, f32[2,256]{1,0:...) while((s32[]{:T(128)}, ...), condition=%wide.region_27.28_spmd.clone, body=%wide.region_0.27_spmd.clone.sunk | while | flops 22718711808 | bytes 744419392 | solution.py:264
  151.7 23.2 %all-gather.10.cloned.1.call-done = bf16[1024,1,1024]{2,0,1:T(8,128)(2,1)} async-done(((bf16[256,1,1024]{2,0,1:T(8,128)(2,1)}), bf16[1024,1,1024]{2,0,1:T(8,128)(2,1)}) %all-gather.10.cloned.1.call-update) | async-done | bytes 2097168 | tf_op jit(solution)/shard_map/while/body/eval_jaxpr/all_gather | solution.py:155
  196.7 44.7 %reduce-scatter.8.cloned.1.call-done = f32[256,1,1024]{2,0,1:T(8,128)} async-done(((f32[1024,1,1024]{2,0,1:T(8,128)}), f32[256,1,1024]{2,0,1:T(8,128)}) %reduce-scatter.8.cloned.1.call-update) | async-done | bytes 1048592 | tf_op jit(solution)/shard_map/while/body/eval_jaxpr/reduce_scatter | solution.py:169
  244.5 22.4 %all-gather.12.cloned.1.call-done = bf16[1024,1,1024]{2,0,1:T(8,128)(2,1)} async-done(((bf16[256,1,1024]{2,0,1:T(8,128)(2,1)}), bf16[1024,1,1024]{2,0,1:T(8,128)(2,1)}) %all-gather.12.cloned.1.call-update) | async-done | bytes 2097168 | tf_op jit(solution)/shard_map/while/body/eval_jaxpr/all_gather | solution.py:178
  271.6 5.7 convert_reduce_fusion.9
  283.1 44.7 %reduce-scatter.12.cloned.1.call-done = f32[256,1,1024]{2,0,1:T(8,128)} async-done(((f32[1024,1,1024]{2,0,1:T(8,128)}), f32[256,1,1024]{2,0,1:T(8,128)}) %reduce-scatter.12.cloned.1.call-update) | async-done | bytes 1048592 | tf_op jit(solution)/shard_map/while/body/eval_jaxpr/reduce_scatter | solution.py:205
  332.3 7.0 convert_bitcast_fusion.4
  339.8 15.1 %all-gather.14.cloned.1.call-done = bf16[1024,1,1024]{2,0,1:T(8,128)(2,1)} async-done(((bf16[256,1,1024]{2,0,1:T(8,128)(2,1)}), bf16[1024,1,1024]{2,0,1:T(8,128)(2,1)}) %all-gather.14.cloned.1.call-update) | async-done | bytes 2097168 | tf_op jit(solution)/shard_map/while/body/eval_jaxpr/all_gather | solution.py:216
  362.4 7.6 multiply_reduce_fusion.13
  374.6 6.8 multiply_convert_fusion.11
  384.3 5.5 multiply_reduce_fusion.14
  405.1 5.7 convolution_bitcast_fusion.8
  411.9 6.7 fusion.227
  438.5 5.7 maximum_add_fusion.4
  444.2 11.6 %reduce-scatter.14.cloned.1.call-done = f32[256,1,1024]{2,0,1:T(8,128)} async-done(((f32[1024,1,1024]{2,0,1:T(8,128)}), f32[256,1,1024]{2,0,1:T(8,128)}) %reduce-scatter.14.cloned.1.call-update) | async-done | bytes 1048592 | tf_op jit(solution)/shard_map/while/body/eval_jaxpr/reduce_scatter | solution.py:234
  462.6 22.9 %all-gather.10.cloned.1.call-done = bf16[1024,1,1024]{2,0,1:T(8,128)(2,1)} async-done(((bf16[256,1,1024]{2,0,1:T(8,128)(2,1)}), bf16[1024,1,1024]{2,0,1:T(8,128)(2,1)}) %all-gather.10.cloned.1.call-update) | async-done | bytes 2097168 | tf_op jit(solution)/shard_map/while/body/eval_jaxpr/all_gather | solution.py:155
  507.3 44.7 %reduce-scatter.8.cloned.1.call-done = f32[256,1,1024]{2,0,1:T(8,128)} async-done(((f32[1024,1,1024]{2,0,1:T(8,128)}), f32[256,1,1024]{2,0,1:T(8,128)}) %reduce-scatter.8.cloned.1.call-update) | async-done | bytes 1048592 | tf_op jit(solution)/shard_map/while/body/eval_jaxpr/reduce_scatter | solution.py:169
  555.3 22.2 %all-gather.12.cloned.1.call-done = bf16[1024,1,1024]{2,0,1:T(8,128)(2,1)} async-done(((bf16[256,1,1024]{2,0,1:T(8,128)(2,1)}), bf16[1024,1,1024]{2,0,1:T(8,128)(2,1)}) %all-gather.12.cloned.1.call-update) | async-done | bytes 2097168 | tf_op jit(solution)/shard_map/while/body/eval_jaxpr/all_gather | solution.py:178
  582.2 5.7 convert_reduce_fusion.9
  593.7 44.7 %reduce-scatter.12.cloned.1.call-done = f32[256,1,1024]{2,0,1:T(8,128)} async-done(((f32[1024,1,1024]{2,0,1:T(8,128)}), f32[256,1,1024]{2,0,1:T(8,128)}) %reduce-scatter.12.cloned.1.call-update) | async-done | bytes 1048592 | tf_op jit(solution)/shard_map/while/body/eval_jaxpr/reduce_scatter | solution.py:205
  642.9 7.0 convert_bitcast_fusion.4
  650.1 15.4 %all-gather.14.cloned.1.call-done = bf16[1024,1,1024]{2,0,1:T(8,128)(2,1)} async-done(((bf16[256,1,1024]{2,0,1:T(8,128)(2,1)}), bf16[1024,1,1024]{2,0,1:T(8,128)(2,1)}) %all-gather.14.cloned.1.call-update) | async-done | bytes 2097168 | tf_op jit(solution)/shard_map/while/body/eval_jaxpr/all_gather | solution.py:216
  673.0 7.6 multiply_reduce_fusion.13
  685.1 6.8 multiply_convert_fusion.11
  715.7 5.7 convolution_bitcast_fusion.8
  722.5 6.7 fusion.227
  749.2 10.1 %maximum_add_fusion.4 = f32[1024,3072]{0,1:T(8,128)} fusion(f32[1024,1024]{0,1:T(8,128)S(1)} %copy-done.11, f32[1024,1024]{0,1:T(8,128)S(1)} %copy-done.10, f32[1024,256]{0,1:T(8,128)S(1)} %fusion.228, f32[1024,768]{0,1:T(8,128)S(1)} %fusion.230, f32[1024,3072]{0,1:T(8,128)} %get-tuple-element.947, pred[]{:T(512)S(6)} %compare.3), kind=kLoop, calls=%fused_computation.clone.1 | loop fusion | flops 15728640 | bytes 37748736 | tf_op jit(solution)/shard_map/while/body/eval_jaxpr/add | solution.py:248
  759.3 7.1 reduce-scatter.14.cloned.1.call-done
  773.7 43.1 %psum.7 = f32[12288]{0:T(1024)S(1)} all-reduce(f32[12288]{0:T(1024)S(1)} %constant_dynamic-update-slice_fusion), channel_id=1, replica_groups=mesh['dp'=8,'tensor'=4] {'dp','tensor'}, use_global_device_ids=true, to_apply=%region_29.30 | all-reduce | flops 12288 | bytes 98304 | tf_op jit(solution)/shard_map/psum | solution.py:278
  818.7 167.7 %reduce-scatter.6.cloned.1.call-done = f32[128,3072]{0,1:T(8,128)} async-done(((f32[1024,3072]{0,1:T(8,128)}), f32[128,3072]{0,1:T(8,128)}) %reduce-scatter.6.cloned.1.call-update) | async-done | bytes 1572880 | tf_op jit(solution)/shard_map/reduce_scatter | solution.py:267
  (354 shorter events, 230.4 us)
Async XLA Ops:
  7.2 107.7 %all-gather.6.cloned.1.call-start = ((), (), s32[]{:S(2)}) async-start(), calls=%async_computation.5 | async-start | bytes 7077888 | tf_op jit(solution)/shard_map/all_gather | solution.py:125
  12.5 136.6 %all-gather.8.cloned.1.call-start = ((), (), s32[]{:S(2)}) async-start(), calls=%async_computation.6 | async-start | bytes 5242880 | tf_op jit(solution)/shard_map/all_gather | solution.py:131
  122.7 26.3 %copy-start.5 = (bf16[2,256,1,1024]{3,1,2,0:T(8,128)(2,1)S(1)}, bf16[2,256,1,1024]{3,1,2,0:T(8,128)(2,1)}, u32[]{:S(2)}) copy-start(bf16[2,256,1,1024]{3,1,2,0:T(8,128)(2,1)} %param.16) | copy-start | bytes 3145732
  122.7 26.3 %copy-start.20 = (f32[1024]{0:T(1024)S(1)}, f32[1024]{0:T(1024)}, u32[]{:S(2)}) copy-start(f32[1024]{0:T(1024)} %param.25) | copy-start | bytes 12292
  122.7 26.3 %copy-start.21 = (f32[1024]{0:T(1024)S(1)}, f32[1024]{0:T(1024)}, u32[]{:S(2)}) copy-start(f32[1024]{0:T(1024)} %param.27) | copy-start | bytes 12292
  122.7 26.3 %copy-start.22 = (f32[1024]{0:T(1024)S(1)}, f32[1024]{0:T(1024)}, u32[]{:S(2)}) copy-start(f32[1024]{0:T(1024)} %param.26) | copy-start | bytes 12292
  122.8 26.3 %copy-start.23 = (f32[1024]{0:T(1024)S(1)}, f32[1024]{0:T(1024)}, u32[]{:S(2)}) copy-start(f32[1024]{0:T(1024)} %param.20) | copy-start | bytes 12292
  122.8 26.3 %copy-start.24 = (f32[1024]{0:T(1024)S(1)}, f32[1024]{0:T(1024)}, u32[]{:S(2)}) copy-start(f32[1024]{0:T(1024)} %param.28) | copy-start | bytes 12292
  122.8 26.3 %copy-start.25 = (f32[1024]{0:T(1024)S(1)}, f32[1024]{0:T(1024)}, u32[]{:S(2)}) copy-start(f32[1024]{0:T(1024)} %param.24) | copy-start | bytes 12292
  122.8 26.3 %copy-start.26 = (f32[2,256]{1,0:T(2,128)S(1)}, f32[2,256]{1,0:T(2,128)}, u32[]{:S(2)}) copy-start(f32[2,256]{1,0:T(2,128)} %param.18) | copy-start | bytes 6148
  122.8 26.3 %copy-start.30 = (f32[1024]{0:T(1024)S(1)}, f32[1024]{0:T(1024)}, u32[]{:S(2)}) copy-start(f32[1024]{0:T(1024)} %param.22) | copy-start | bytes 12292
  149.4 43.9 %copy-start.16 = (bf16[1024,256]{1,0:T(8,128)(2,1)}, bf16[1024,256]{1,0:T(8,128)(2,1)S(1)}, u32[]{:S(2)}) copy-start(bf16[1024,256]{1,0:T(8,128)(2,1)S(1)} %get-tuple-element.992) | copy-start | bytes 1572868 | tf_op jit(solution)/shard_map/while
  149.4 25.5 %all-gather.10.cloned.1.call-start = ((), (), s32[]{:S(2)}) async-start(), calls=%async_computation.8 | async-start | bytes 2621440 | tf_op jit(solution)/shard_map/while/body/eval_jaxpr/all_gather | solution.py:155
  151.0 90.4 %reduce-scatter.8.cloned.1.call-start = ((), (), s32[]{:S(2)}) async-start(), calls=%async_computation.9 | async-start | bytes 5242880 | tf_op jit(solution)/shard_map/while/body/eval_jaxpr/reduce_scatter | solution.py:169
  196.6 70.3 %all-gather.12.cloned.1.call-start = ((), (), s32[]{:S(2)}) async-start(), calls=%async_computation.10 | async-start | bytes 2621440 | tf_op jit(solution)/shard_map/while/body/eval_jaxpr/all_gather | solution.py:178
  244.1 83.6 %reduce-scatter.12.cloned.1.call-start = ((), (), s32[]{:S(2)}) async-start(), calls=%async_computation.12 | async-start | bytes 5242880 | tf_op jit(solution)/shard_map/while/body/eval_jaxpr/reduce_scatter | solution.py:205
  283.0 71.9 %all-gather.14.cloned.1.call-start = ((), (), s32[]{:S(2)}) async-start(), calls=%async_computation.13 | async-start | bytes 2621440 | tf_op jit(solution)/shard_map/while/body/eval_jaxpr/all_gather | solution.py:216
  332.2 91.3 %reduce-scatter.10.cloned.1.call-start = ((), (), s32[]{:S(2)}) async-start(), calls=%async_computation.11 | async-start | bytes 2621440 | tf_op jit(solution)/shard_map/while/body/eval_jaxpr/reduce_scatter | solution.py:184
  339.3 116.5 %reduce-scatter.14.cloned.1.call-start = ((), (), s32[]{:S(2)}) async-start(), calls=%async_computation.14 | async-start | bytes 5242880 | tf_op jit(solution)/shard_map/while/body/eval_jaxpr/reduce_scatter | solution.py:234
  357.4 12.7 %slice-start.2 = ((s8[8388608]{0:T(1024)(128)(4,1)}), s8[4194304]{0:T(1024)(128)(4,1)S(1)}, s32[]{:S(2)}) async-start(s8[8388608]{0:T(1024)(128)(4,1)} %bitcast.324), calls=%async_computation.17 | async-start | bytes 8388608 | tf_op jit(solution)/shard_map/while
  444.2 15.8 %copy-start.17 = (bf16[1024,256]{1,0:T(8,128)(2,1)S(1)}, bf16[1024,256]{1,0:T(8,128)(2,1)}, u32[]{:S(2)}) copy-start(bf16[1024,256]{1,0:T(8,128)(2,1)} %copy-done.16) | copy-start | bytes 1572868 | tf_op jit(solution)/shard_map/while
  460.3 43.6 %copy-start.16 = (bf16[1024,256]{1,0:T(8,128)(2,1)}, bf16[1024,256]{1,0:T(8,128)(2,1)S(1)}, u32[]{:S(2)}) copy-start(bf16[1024,256]{1,0:T(8,128)(2,1)S(1)} %get-tuple-element.992) | copy-start | bytes 1572868 | tf_op jit(solution)/shard_map/while
  460.3 25.2 %all-gather.10.cloned.1.call-start = ((), (), s32[]{:S(2)}) async-start(), calls=%async_computation.8 | async-start | bytes 2621440 | tf_op jit(solution)/shard_map/while/body/eval_jaxpr/all_gather | solution.py:155
  461.9 90.1 %reduce-scatter.8.cloned.1.call-start = ((), (), s32[]{:S(2)}) async-start(), calls=%async_computation.9 | async-start | bytes 5242880 | tf_op jit(solution)/shard_map/while/body/eval_jaxpr/reduce_scatter | solution.py:169
  507.2 70.3 %all-gather.12.cloned.1.call-start = ((), (), s32[]{:S(2)}) async-start(), calls=%async_computation.10 | async-start | bytes 2621440 | tf_op jit(solution)/shard_map/while/body/eval_jaxpr/all_gather | solution.py:178
  554.8 83.6 %reduce-scatter.12.cloned.1.call-start = ((), (), s32[]{:S(2)}) async-start(), calls=%async_computation.12 | async-start | bytes 5242880 | tf_op jit(solution)/shard_map/while/body/eval_jaxpr/reduce_scatter | solution.py:205
  593.6 71.9 %all-gather.14.cloned.1.call-start = ((), (), s32[]{:S(2)}) async-start(), calls=%async_computation.13 | async-start | bytes 2621440 | tf_op jit(solution)/shard_map/while/body/eval_jaxpr/all_gather | solution.py:216
  642.8 91.3 %reduce-scatter.10.cloned.1.call-start = ((), (), s32[]{:S(2)}) async-start(), calls=%async_computation.11 | async-start | bytes 2621440 | tf_op jit(solution)/shard_map/while/body/eval_jaxpr/reduce_scatter | solution.py:184
  649.9 116.5 %reduce-scatter.14.cloned.1.call-start = ((), (), s32[]{:S(2)}) async-start(), calls=%async_computation.14 | async-start | bytes 5242880 | tf_op jit(solution)/shard_map/while/body/eval_jaxpr/reduce_scatter | solution.py:234
  668.0 12.7 %slice-start.2 = ((s8[8388608]{0:T(1024)(128)(4,1)}), s8[4194304]{0:T(1024)(128)(4,1)S(1)}, s32[]{:S(2)}) async-start(s8[8388608]{0:T(1024)(128)(4,1)} %bitcast.324), calls=%async_computation.17 | async-start | bytes 8388608 | tf_op jit(solution)/shard_map/while
  759.3 11.3 %copy-start.17 = (bf16[1024,256]{1,0:T(8,128)(2,1)S(1)}, bf16[1024,256]{1,0:T(8,128)(2,1)}, u32[]{:S(2)}) copy-start(bf16[1024,256]{1,0:T(8,128)(2,1)} %copy-done.16) | copy-start | bytes 1572868 | tf_op jit(solution)/shard_map/while
  772.8 213.5 %reduce-scatter.6.cloned.1.call-start = ((), (), s32[]{:S(2)}) async-start(), calls=%async_computation.7 | async-start | bytes 14155776 | tf_op jit(solution)/shard_map/reduce_scatter | solution.py:267
  (54 other events, 267.1 us)
Sparse Core Ops, SparseCore 0:
  12.6 102.1 all-gather.5
  116.4 32.6 all-gather.7
  152.3 22.5 all-gather.9
  196.7 44.5 reduce-scatter.7
  244.3 22.5 all-gather.11
  283.1 44.5 reduce-scatter.11
  332.3 22.5 all-gather.13
  357.4 31.1 reduce-scatter.9
  410.9 44.8 reduce-scatter.13
  462.9 22.5 all-gather.9
  507.3 44.5 reduce-scatter.7
  554.9 22.5 all-gather.11
  593.7 44.5 reduce-scatter.11
  642.9 22.5 all-gather.13
  667.9 31.1 reduce-scatter.9
  721.5 44.8 reduce-scatter.13
  776.9 209.3 reduce-scatter.5
where the time goes:
time: 1000 us; the launch traced here: 999 us
  waiting for transfers between devices  608 us (61%)
  matrix products  180 us (18%)
  other arithmetic  85.3 us (9%)
  local copies, waits for them, and re-layouts  62.5 us (6%)
  blocking collectives  43.1 us (4%)
  between operations  14.7 us (1%)
    reduce_scatter x1, waiting for transfers between devices, per_device(): lax.psum_scatter(weight_acc, 'dp', scatter_dimension=0, tiled=True)  168 us
    all_gather x1, waiting for transfers between devices, per_device(): packed_full = lax.all_gather(packed, 'dp', axis=0, tiled=True)  101 us
    reduce_scatter x2, waiting for transfers between devices, one_micro(): lax.psum_scatter(jnp.einsum('lbi,oi->lbo', mixed, out_full, preferred_ele...  89.4 us
    reduce_scatter x2, waiting for transfers between devices, one_micro(): lax.psum_scatter(jnp.einsum('lbf,df->lbd', grad_pre, fc_full, preferred_e...  89.3 us
    all_gather x2, waiting for transfers between devices, one_micro(): hidden1_full = lax.all_gather(hidden1, 'tensor', axis=0, tiled=True)  46.1 us
    all_gather x2, waiting for transfers between devices, one_micro(): hidden2_full = lax.all_gather(hidden2, 'tensor', axis=0, tiled=True)  44.6 us
    psum x1, blocking collectives, per_device(): lax.psum(jnp.concatenate([feature_vec, head_slots.reshape(-1)]), ('dp', '...  43.1 us
    all_gather x2, waiting for transfers between devices, one_micro(): lax.all_gather(grad_mid.astype(jnp.bfloat16), 'tensor', axis=0, tiled=True)  30.5 us
  transfers between devices with their start and end apart: 17, of which 15 were waited for; matrix products, arithmetic and copies ran while one was open for 21% of the time, Pallas kernels for 0%

commit v1 on v0

--- a/solution.py
+++ b/solution.py
@@ -8,6 +8,27 @@
 tanh_coef = 0.7978845608028654
 cube_coef = 0.044715
 block_rows = 512
+
+
+def gather_around(array, axis, dim):
+    size, index, rows = (lax.axis_size(axis), lax.axis_index(axis), array.shape[dim])
+    upward = [(i, (i + 1) % size) for i in range(size)]
+    backward = [(i, (i - 1) % size) for i in range(size)]
+    result = jnp.zeros((*array.shape[:dim], size * rows, *array.shape[dim + 1 :]), array.dtype)
+    result = lax.dynamic_update_slice_in_dim(result, array, index * rows, axis=dim)
+    from_left = from_right = array
+    half = size // 2
+    for lap in range(1, half + 1):
+        from_left = lax.ppermute(from_left, axis, upward)
+        result = lax.dynamic_update_slice_in_dim(
+            result, from_left, (index - lap) % size * rows, axis=dim
+        )
+        if lap < size - half:
+            from_right = lax.ppermute(from_right, axis, backward)
+            result = lax.dynamic_update_slice_in_dim(
+                result, from_right, (index + lap) % size * rows, axis=dim
+            )
+    return result
 
 
 def gelu_tanh(values):
@@ -122,7 +143,7 @@
     packed = jnp.concatenate(
         [qkv_weight.reshape(rows, width_qkv), out_weight, fc_weight, proj_weight], axis=1
     )
-    packed_full = lax.all_gather(packed, "dp", axis=0, tiled=True)
+    packed_full = gather_around(packed, "dp", 0)
     depth = packed_full.shape[0]
     qkv_full = packed_full[:, : cuts[0]].reshape(depth, 3, qkv_weight.shape[2])
     out_full = packed_full[:, cuts[0] : cuts[1]]

time: 1000 us -> 1020 us (1.020)
  waiting for transfers between devices: 608 us -> 588 us
  starting transfers between devices: 2.08 us -> 21.8 us
  local copies, waits for them, and re-layouts: 62.5 us -> 74.9 us
    ppermute x0 -> x7, waiting for transfers between devices: none -> 102 us  [the longest x4 86.1 us: gather_around(): from_left = lax.ppermute(from_left, axis, upward)]
    all_gather x1 -> x0, waiting for transfers between devices: 101 us -> none  [per_device(): packed_full = lax.all_gather(packed, 'dp', axis=0, tiled=True)]
    ppermute x0 -> x7, starting transfers between devices: none -> 19.7 us  [the longest x4 10.4 us: gather_around(): from_left = lax.ppermute(from_left, axis, upward)]
    all_gather x1, waiting for transfers between devices: 19 us -> 0.01 us  [per_device(): grad_top_all = lax.all_gather(out_grad, 'tensor', axis=1, tiled=True)]
  transfers between devices with their start and end apart: 17 -> 23, of which waited for: 15 -> 17; matrix products, arithmetic and copies ran while one was open for 21% -> 22% of each run, Pallas kernels for 0% -> 0%
where the time goes in v1:
time: 1020 us; the launch traced here: 1010 us
  waiting for transfers between devices  588 us (58%)
  matrix products  180 us (18%)
  other arithmetic  85.3 us (8%)
  local copies, waits for them, and re-layouts  74.9 us (7%)
  blocking collectives  43 us (4%)
  starting transfers between devices  21.8 us (2%)
  between operations  14.7 us (1%)
    reduce_scatter x1, waiting for transfers between devices, per_device(): lax.psum_scatter(weight_acc, 'dp', scatter_dimension=0, tiled=True)  168 us
    reduce_scatter x2, waiting for transfers between devices, one_micro(): lax.psum_scatter(jnp.einsum('lbi,oi->lbo', mixed, out_full, preferred_ele...  89.4 us
    reduce_scatter x2, waiting for transfers between devices, one_micro(): lax.psum_scatter(jnp.einsum('lbf,df->lbd', grad_pre, fc_full, preferred_e...  89.3 us
    ppermute x4, waiting for transfers between devices, gather_around(): from_left = lax.ppermute(from_left, axis, upward)  86.1 us
    all_gather x2, waiting for transfers between devices, one_micro(): hidden2_full = lax.all_gather(hidden2, 'tensor', axis=0, tiled=True)  44.6 us
    all_gather x2, waiting for transfers between devices, one_micro(): hidden1_full = lax.all_gather(hidden1, 'tensor', axis=0, tiled=True)  43.8 us
    psum x1, blocking collectives, per_device(): lax.psum(jnp.concatenate([feature_vec, head_slots.reshape(-1)]), ('dp', '...  43 us
    all_gather x2, waiting for transfers between devices, one_micro(): lax.all_gather(grad_mid.astype(jnp.bfloat16), 'tensor', axis=0, tiled=True)  30.5 us
  transfers between devices with their start and end apart: 23, of which 17 were waited for; matrix products, arithmetic and copies ran while one was open for 22% of the time, Pallas kernels for 0%

profile of v1, /device:TPU:0, one launch (start us, length us, event | category | flops | bytes accessed | tf_op | source)
XLA Modules:
  0.0 1010.9 jit_solution(15744067232532264027)
XLA Ops:
  22.8 30.6 %collective-permute-done = bf16[128,3072]{0,1:T(8,128)(2,1)S(1)} collective-permute-done((bf16[128,3072]{0,1:T(8,128)(2,1)S(1)}, bf16[128,3072]{0,1:T(8,128)(2,1)S(1)}, u32[]{:S(2)}, u32[]{:S(2)}) %collective-permute-start) | collective-permute-done | bytes 786464 | tf_op jit(solution)/shard_map/ppermute | solution.py:22
  59.0 29.6 %collective-permute-done.2 = bf16[128,3072]{0,1:T(8,128)(2,1)S(1)} collective-permute-done((bf16[128,3072]{0,1:T(8,128)(2,1)S(1)}, bf16[128,3072]{0,1:T(8,128)(2,1)S(1)}, u32[]{:S(2)}, u32[]{:S(2)}) %collective-permute-start.2) | collective-permute-done | bytes 786464 | tf_op jit(solution)/shard_map/ppermute | solution.py:22
  97.3 25.9 %collective-permute-done.4 = bf16[128,3072]{0,1:T(8,128)(2,1)S(1)} collective-permute-done((bf16[128,3072]{0,1:T(8,128)(2,1)S(1)}, bf16[128,3072]{0,1:T(8,128)(2,1)S(1)}, u32[]{:S(2)}, u32[]{:S(2)}) %collective-permute-start.4) | collective-permute-done | bytes 786464 | tf_op jit(solution)/shard_map/ppermute | solution.py:22
  127.6 16.1 %collective-permute-done.5 = bf16[128,3072]{0,1:T(8,128)(2,1)S(1)} collective-permute-done((bf16[128,3072]{0,1:T(8,128)(2,1)S(1)}, bf16[128,3072]{0,1:T(8,128)(2,1)S(1)}, u32[]{:S(2)}, u32[]{:S(2)}) %collective-permute-start.5) | collective-permute-done | bytes 786464 | tf_op jit(solution)/shard_map/ppermute | solution.py:27
  163.0 621.4 %while.34 = (s32[]{:T(128)}, bf16[2,256,1,1024]{3,1,2,0:T(8,128)(2,1)}, bf16[2,256,1,1024]{3,1,2,0:T(8,128)(2,1)}, f32[1024,3072]{0,1:T(8,128)}, f32[2,256]{1,0:...) while((s32[]{:T(128)}, ...), condition=%wide.region_27.28_spmd.clone, body=%wide.region_0.27_spmd.clone.sunk | while | flops 22718711808 | bytes 744419392 | solution.py:285
  165.6 20.6 %all-gather.7.cloned.1.call-done = bf16[1024,1,1024]{2,0,1:T(8,128)(2,1)} async-done(((bf16[256,1,1024]{2,0,1:T(8,128)(2,1)}), bf16[1024,1,1024]{2,0,1:T(8,128)(2,1)}) %all-gather.7.cloned.1.call-update) | async-done | bytes 2097168 | tf_op jit(solution)/shard_map/while/body/eval_jaxpr/all_gather | solution.py:176
  208.0 44.7 %reduce-scatter.8.cloned.1.call-done = f32[256,1,1024]{2,0,1:T(8,128)} async-done(((f32[1024,1,1024]{2,0,1:T(8,128)}), f32[256,1,1024]{2,0,1:T(8,128)}) %reduce-scatter.8.cloned.1.call-update) | async-done | bytes 1048592 | tf_op jit(solution)/shard_map/while/body/eval_jaxpr/reduce_scatter | solution.py:190
  255.7 22.4 %all-gather.9.cloned.1.call-done = bf16[1024,1,1024]{2,0,1:T(8,128)(2,1)} async-done(((bf16[256,1,1024]{2,0,1:T(8,128)(2,1)}), bf16[1024,1,1024]{2,0,1:T(8,128)(2,1)}) %all-gather.9.cloned.1.call-update) | async-done | bytes 2097168 | tf_op jit(solution)/shard_map/while/body/eval_jaxpr/all_gather | solution.py:199
  282.9 5.7 convert_reduce_fusion.9
  294.4 44.7 %reduce-scatter.12.cloned.1.call-done = f32[256,1,1024]{2,0,1:T(8,128)} async-done(((f32[1024,1,1024]{2,0,1:T(8,128)}), f32[256,1,1024]{2,0,1:T(8,128)}) %reduce-scatter.12.cloned.1.call-update) | async-done | bytes 1048592 | tf_op jit(solution)/shard_map/while/body/eval_jaxpr/reduce_scatter | solution.py:226
  343.6 7.0 convert_bitcast_fusion.4
  351.1 15.1 %all-gather.11.cloned.1.call-done = bf16[1024,1,1024]{2,0,1:T(8,128)(2,1)} async-done(((bf16[256,1,1024]{2,0,1:T(8,128)(2,1)}), bf16[1024,1,1024]{2,0,1:T(8,128)(2,1)}) %all-gather.11.cloned.1.call-update) | async-done | bytes 2097168 | tf_op jit(solution)/shard_map/while/body/eval_jaxpr/all_gather | solution.py:237
  373.7 7.6 multiply_reduce_fusion.13
  385.9 6.8 multiply_convert_fusion.11
  416.3 5.6 convolution_bitcast_fusion.8
  423.2 6.7 fusion.228
  455.4 11.7 %reduce-scatter.14.cloned.1.call-done = f32[256,1,1024]{2,0,1:T(8,128)} async-done(((f32[1024,1,1024]{2,0,1:T(8,128)}), f32[256,1,1024]{2,0,1:T(8,128)}) %reduce-scatter.14.cloned.1.call-update) | async-done | bytes 1048592 | tf_op jit(solution)/shard_map/while/body/eval_jaxpr/reduce_scatter | solution.py:255
  473.9 23.2 %all-gather.7.cloned.1.call-done = bf16[1024,1,1024]{2,0,1:T(8,128)(2,1)} async-done(((bf16[256,1,1024]{2,0,1:T(8,128)(2,1)}), bf16[1024,1,1024]{2,0,1:T(8,128)(2,1)}) %all-gather.7.cloned.1.call-update) | async-done | bytes 2097168 | tf_op jit(solution)/shard_map/while/body/eval_jaxpr/all_gather | solution.py:176
  518.8 44.7 %reduce-scatter.8.cloned.1.call-done = f32[256,1,1024]{2,0,1:T(8,128)} async-done(((f32[1024,1,1024]{2,0,1:T(8,128)}), f32[256,1,1024]{2,0,1:T(8,128)}) %reduce-scatter.8.cloned.1.call-update) | async-done | bytes 1048592 | tf_op jit(solution)/shard_map/while/body/eval_jaxpr/reduce_scatter | solution.py:190
  566.9 22.2 %all-gather.9.cloned.1.call-done = bf16[1024,1,1024]{2,0,1:T(8,128)(2,1)} async-done(((bf16[256,1,1024]{2,0,1:T(8,128)(2,1)}), bf16[1024,1,1024]{2,0,1:T(8,128)(2,1)}) %all-gather.9.cloned.1.call-update) | async-done | bytes 2097168 | tf_op jit(solution)/shard_map/while/body/eval_jaxpr/all_gather | solution.py:199
  593.8 5.7 convert_reduce_fusion.9
  605.3 44.7 %reduce-scatter.12.cloned.1.call-done = f32[256,1,1024]{2,0,1:T(8,128)} async-done(((f32[1024,1,1024]{2,0,1:T(8,128)}), f32[256,1,1024]{2,0,1:T(8,128)}) %reduce-scatter.12.cloned.1.call-update) | async-done | bytes 1048592 | tf_op jit(solution)/shard_map/while/body/eval_jaxpr/reduce_scatter | solution.py:226
  654.5 7.0 convert_bitcast_fusion.4
  661.7 15.4 %all-gather.11.cloned.1.call-done = bf16[1024,1,1024]{2,0,1:T(8,128)(2,1)} async-done(((bf16[256,1,1024]{2,0,1:T(8,128)(2,1)}), bf16[1024,1,1024]{2,0,1:T(8,128)(2,1)}) %all-gather.11.cloned.1.call-update) | async-done | bytes 2097168 | tf_op jit(solution)/shard_map/while/body/eval_jaxpr/all_gather | solution.py:237
  684.6 7.6 multiply_reduce_fusion.13
  696.7 6.8 multiply_convert_fusion.11
  727.2 5.6 convolution_bitcast_fusion.8
  734.1 6.7 fusion.228
  760.7 10.1 maximum_add_fusion.4
  770.8 7.2 reduce-scatter.14.cloned.1.call-done
  785.3 43.0 %psum.7 = f32[12288]{0:T(1024)S(1)} all-reduce(f32[12288]{0:T(1024)S(1)} %constant_dynamic-update-slice_fusion), channel_id=1, replica_groups=mesh['dp'=8,'tensor'=4] {'dp','tensor'}, use_global_device_ids=true, to_apply=%region_29.30 | all-reduce | flops 12288 | bytes 98304 | tf_op jit(solution)/shard_map/psum | solution.py:299
  830.2 167.7 %reduce-scatter.6.cloned.1.call-done = f32[128,3072]{0,1:T(8,128)} async-done(((f32[1024,3072]{0,1:T(8,128)}), f32[128,3072]{0,1:T(8,128)}) %reduce-scatter.6.cloned.1.call-update) | async-done | bytes 1572880 | tf_op jit(solution)/shard_map/reduce_scatter | solution.py:288
  (372 shorter events, 273.7 us)
Async XLA Ops:
  7.2 155.7 %all-gather.5.cloned.1.call-start = ((), (), s32[]{:S(2)}) async-start(), calls=%async_computation.5 | async-start | bytes 5242880 | tf_op jit(solution)/shard_map/all_gather | solution.py:152
  16.7 36.6 %collective-permute-start = (bf16[128,3072]{0,1:T(8,128)(2,1)S(1)}, bf16[128,3072]{0,1:T(8,128)(2,1)S(1)}, u32[]{:S(2)}, u32[]{:S(2)}) collective-permute-start(bf16[128,3072]{0,1:T(8,128)(2,1)S(1)} %get-tuple-element.676), channel_id=1, source_target_pairs={{0,4},{4,8},{8,12},{12,16},{16,20},{20,24},{24,28},{28,0},{1,5},{5... | collective-permute-start | bytes 2359304 | tf_op jit(solution)/shard_map/ppermute | solution.py:22
  19.7 36.1 %collective-permute-start.1 = (bf16[128,3072]{0,1:T(8,128)(2,1)S(1)}, bf16[128,3072]{0,1:T(8,128)(2,1)S(1)}, u32[]{:S(2)}, u32[]{:S(2)}) collective-permute-start(bf16[128,3072]{0,1:T(8,128)(2,1)S(1)} %get-tuple-element.676), channel_id=1, source_target_pairs={{0,28},{4,0},{8,4},{12,8},{16,12},{20,16},{24,20},{28,24},{1,29},{... | collective-permute-start | bytes 2359304 | tf_op jit(solution)/shard_map/ppermute | solution.py:27
  53.3 35.3 %collective-permute-start.2 = (bf16[128,3072]{0,1:T(8,128)(2,1)S(1)}, bf16[128,3072]{0,1:T(8,128)(2,1)S(1)}, u32[]{:S(2)}, u32[]{:S(2)}) collective-permute-start(bf16[128,3072]{0,1:T(8,128)(2,1)S(1)} %collective-permute-done), channel_id=1, source_target_pairs={{0,4},{4,8},{8,12},{12,16},{16,20},{20,24},{24,28},{28,0},{1,5},{5... | collective-permute-start | bytes 2359304 | tf_op jit(solution)/shard_map/ppermute | solution.py:22
  55.8 37.3 %collective-permute-start.3 = (bf16[128,3072]{0,1:T(8,128)(2,1)S(1)}, bf16[128,3072]{0,1:T(8,128)(2,1)S(1)}, u32[]{:S(2)}, u32[]{:S(2)}) collective-permute-start(bf16[128,3072]{0,1:T(8,128)(2,1)S(1)} %collective-permute-done.1), channel_id=1, source_target_pairs={{0,28},{4,0},{8,4},{12,8},{16,12},{20,16},{24,20},{28,24},{1,29},{... | collective-permute-start | bytes 2359304 | tf_op jit(solution)/shard_map/ppermute | solution.py:27
  88.6 34.6 %collective-permute-start.4 = (bf16[128,3072]{0,1:T(8,128)(2,1)S(1)}, bf16[128,3072]{0,1:T(8,128)(2,1)S(1)}, u32[]{:S(2)}, u32[]{:S(2)}) collective-permute-start(bf16[128,3072]{0,1:T(8,128)(2,1)S(1)} %collective-permute-done.2), channel_id=1, source_target_pairs={{0,4},{4,8},{8,12},{12,16},{16,20},{20,24},{24,28},{28,0},{1,5},{5... | collective-permute-start | bytes 2359304 | tf_op jit(solution)/shard_map/ppermute | solution.py:22
  93.1 50.6 %collective-permute-start.5 = (bf16[128,3072]{0,1:T(8,128)(2,1)S(1)}, bf16[128,3072]{0,1:T(8,128)(2,1)S(1)}, u32[]{:S(2)}, u32[]{:S(2)}) collective-permute-start(bf16[128,3072]{0,1:T(8,128)(2,1)S(1)} %collective-permute-done.3), channel_id=1, source_target_pairs={{0,28},{4,0},{8,4},{12,8},{16,12},{20,16},{24,20},{28,24},{1,29},{... | collective-permute-start | bytes 2359304 | tf_op jit(solution)/shard_map/ppermute | solution.py:27
  123.2 21.5 %collective-permute-start.6 = (bf16[128,3072]{0,1:T(8,128)(2,1)S(1)}, bf16[128,3072]{0,1:T(8,128)(2,1)S(1)}, u32[]{:S(2)}, u32[]{:S(2)}) collective-permute-start(bf16[128,3072]{0,1:T(8,128)(2,1)S(1)} %collective-permute-done.4), channel_id=1, source_target_pairs={{0,4},{4,8},{8,12},{12,16},{16,20},{20,24},{24,28},{28,0},{1,5},{5... | collective-permute-start | bytes 2359304 | tf_op jit(solution)/shard_map/ppermute | solution.py:22
  163.2 41.3 %copy-start.16 = (bf16[1024,256]{1,0:T(8,128)(2,1)}, bf16[1024,256]{1,0:T(8,128)(2,1)S(1)}, u32[]{:S(2)}) copy-start(bf16[1024,256]{1,0:T(8,128)(2,1)S(1)} %get-tuple-element.994) | copy-start | bytes 1572868 | tf_op jit(solution)/shard_map/while
  163.2 23.0 %all-gather.7.cloned.1.call-start = ((), (), s32[]{:S(2)}) async-start(), calls=%async_computation.7 | async-start | bytes 2621440 | tf_op jit(solution)/shard_map/while/body/eval_jaxpr/all_gather | solution.py:176
  164.8 87.8 %reduce-scatter.8.cloned.1.call-start = ((), (), s32[]{:S(2)}) async-start(), calls=%async_computation.8 | async-start | bytes 5242880 | tf_op jit(solution)/shard_map/while/body/eval_jaxpr/reduce_scatter | solution.py:190
  190.1 10.9 %copy-start.7 = (bf16[1024,3,256]{0,2,1:T(8,128)(2,1)}, bf16[1024,3,256]{0,2,1:T(8,128)(2,1)S(1)}, u32[]{:S(2)}) copy-start(bf16[1024,3,256]{0,2,1:T(8,128)(2,1)S(1)} %add_convert_fusion.5) | copy-start | bytes 4718596 | tf_op jit(solution)/shard_map/while
  207.9 70.3 %all-gather.9.cloned.1.call-start = ((), (), s32[]{:S(2)}) async-start(), calls=%async_computation.9 | async-start | bytes 2621440 | tf_op jit(solution)/shard_map/while/body/eval_jaxpr/all_gather | solution.py:199
  255.4 83.6 %reduce-scatter.12.cloned.1.call-start = ((), (), s32[]{:S(2)}) async-start(), calls=%async_computation.11 | async-start | bytes 5242880 | tf_op jit(solution)/shard_map/while/body/eval_jaxpr/reduce_scatter | solution.py:226
  294.3 71.9 %all-gather.11.cloned.1.call-start = ((), (), s32[]{:S(2)}) async-start(), calls=%async_computation.12 | async-start | bytes 2621440 | tf_op jit(solution)/shard_map/while/body/eval_jaxpr/all_gather | solution.py:237
  343.5 91.2 %reduce-scatter.10.cloned.1.call-start = ((), (), s32[]{:S(2)}) async-start(), calls=%async_computation.10 | async-start | bytes 2621440 | tf_op jit(solution)/shard_map/while/body/eval_jaxpr/reduce_scatter | solution.py:205
  350.6 116.5 %reduce-scatter.14.cloned.1.call-start = ((), (), s32[]{:S(2)}) async-start(), calls=%async_computation.13 | async-start | bytes 5242880 | tf_op jit(solution)/shard_map/while/body/eval_jaxpr/reduce_scatter | solution.py:255
  368.7 12.6 %slice-start.2 = ((s8[8388608]{0:T(1024)(128)(4,1)}), s8[4194304]{0:T(1024)(128)(4,1)S(1)}, s32[]{:S(2)}) async-start(s8[8388608]{0:T(1024)(128)(4,1)} %bitcast.324), calls=%async_computation.16 | async-start | bytes 8388608 | tf_op jit(solution)/shard_map/while
  385.9 8.8 copy-start.8
  455.4 15.9 %copy-start.17 = (bf16[1024,256]{1,0:T(8,128)(2,1)S(1)}, bf16[1024,256]{1,0:T(8,128)(2,1)}, u32[]{:S(2)}) copy-start(bf16[1024,256]{1,0:T(8,128)(2,1)} %copy-done.16) | copy-start | bytes 1572868 | tf_op jit(solution)/shard_map/while
  471.5 43.9 %copy-start.16 = (bf16[1024,256]{1,0:T(8,128)(2,1)}, bf16[1024,256]{1,0:T(8,128)(2,1)S(1)}, u32[]{:S(2)}) copy-start(bf16[1024,256]{1,0:T(8,128)(2,1)S(1)} %get-tuple-element.994) | copy-start | bytes 1572868 | tf_op jit(solution)/shard_map/while
  471.5 25.5 %all-gather.7.cloned.1.call-start = ((), (), s32[]{:S(2)}) async-start(), calls=%async_computation.7 | async-start | bytes 2621440 | tf_op jit(solution)/shard_map/while/body/eval_jaxpr/all_gather | solution.py:176
  473.2 90.4 %reduce-scatter.8.cloned.1.call-start = ((), (), s32[]{:S(2)}) async-start(), calls=%async_computation.8 | async-start | bytes 5242880 | tf_op jit(solution)/shard_map/while/body/eval_jaxpr/reduce_scatter | solution.py:190
  501.0 10.9 %copy-start.7 = (bf16[1024,3,256]{0,2,1:T(8,128)(2,1)}, bf16[1024,3,256]{0,2,1:T(8,128)(2,1)S(1)}, u32[]{:S(2)}) copy-start(bf16[1024,3,256]{0,2,1:T(8,128)(2,1)S(1)} %add_convert_fusion.5) | copy-start | bytes 4718596 | tf_op jit(solution)/shard_map/while
  518.8 70.3 %all-gather.9.cloned.1.call-start = ((), (), s32[]{:S(2)}) async-start(), calls=%async_computation.9 | async-start | bytes 2621440 | tf_op jit(solution)/shard_map/while/body/eval_jaxpr/all_gather | solution.py:199
  566.3 83.6 %reduce-scatter.12.cloned.1.call-start = ((), (), s32[]{:S(2)}) async-start(), calls=%async_computation.11 | async-start | bytes 5242880 | tf_op jit(solution)/shard_map/while/body/eval_jaxpr/reduce_scatter | solution.py:226
  605.2 71.9 %all-gather.11.cloned.1.call-start = ((), (), s32[]{:S(2)}) async-start(), calls=%async_computation.12 | async-start | bytes 2621440 | tf_op jit(solution)/shard_map/while/body/eval_jaxpr/all_gather | solution.py:237
  654.4 91.3 %reduce-scatter.10.cloned.1.call-start = ((), (), s32[]{:S(2)}) async-start(), calls=%async_computation.10 | async-start | bytes 2621440 | tf_op jit(solution)/shard_map/while/body/eval_jaxpr/reduce_scatter | solution.py:205
  661.5 116.5 %reduce-scatter.14.cloned.1.call-start = ((), (), s32[]{:S(2)}) async-start(), calls=%async_computation.13 | async-start | bytes 5242880 | tf_op jit(solution)/shard_map/while/body/eval_jaxpr/reduce_scatter | solution.py:255
  679.6 12.6 %slice-start.2 = ((s8[8388608]{0:T(1024)(128)(4,1)}), s8[4194304]{0:T(1024)(128)(4,1)S(1)}, s32[]{:S(2)}) async-start(s8[8388608]{0:T(1024)(128)(4,1)} %bitcast.324), calls=%async_computation.16 | async-start | bytes 8388608 | tf_op jit(solution)/shard_map/while
  770.8 11.4 %copy-start.17 = (bf16[1024,256]{1,0:T(8,128)(2,1)S(1)}, bf16[1024,256]{1,0:T(8,128)(2,1)}, u32[]{:S(2)}) copy-start(bf16[1024,256]{1,0:T(8,128)(2,1)} %copy-done.16) | copy-start | bytes 1572868 | tf_op jit(solution)/shard_map/while
  784.4 213.5 %reduce-scatter.6.cloned.1.call-start = ((), (), s32[]{:S(2)}) async-start(), calls=%async_computation.6 | async-start | bytes 14155776 | tf_op jit(solution)/shard_map/reduce_scatter | solution.py:288
  (59 other events, 294.6 us)
Sparse Core Ops, SparseCore 0:
  9.5 37.1 all-gather.4
  166.2 19.9 all-gather.6
  208.0 44.5 reduce-scatter.7
  255.5 22.5 all-gather.8
  294.4 44.5 reduce-scatter.11
  343.6 22.5 all-gather.10
  368.7 31.1 reduce-scatter.9
  422.1 44.9 reduce-scatter.13
  474.5 22.5 all-gather.6
  518.9 44.5 reduce-scatter.7
  566.5 22.5 all-gather.8
  605.3 44.5 reduce-scatter.11
  654.5 22.5 all-gather.10
  679.5 31.1 reduce-scatter.9
  733.0 44.8 reduce-scatter.13
  788.5 209.3 reduce-scatter.5
